TPU v7x, 32 devices: a whole 2x2x4 slice. The times are simulated.
32 devices in a mesh: seq: 4 (over z), tensor: 2 (over y), fsdp: 4 (over x, core).
Axes of the slice: x: 2, y: 2, z: 4, core: 2. Of those that a mesh axis runs over, the one named last changes fastest.
Arguments:
- hidden_in: bfloat16 [2048, 2048], P(('seq', 'fsdp'), 'tensor'), may hold values from -12 to 12
- out_cotangent: bfloat16 [2048, 2048], P(('seq', 'fsdp'), 'tensor'), may hold values from -6 to 6
- attn_norm_gain: float32 [2048], replicated, may hold values from 0.1 to 1.9
- attn_norm_bias: float32 [2048], replicated, may hold values from -3 to 3
- mlp_norm_gain: float32 [2048], replicated, may hold values from 0.1 to 1.9
- mlp_norm_bias: float32 [2048], replicated, may hold values from -3 to 3
- qkv_weight: bfloat16 [2048, 6144], P(('seq', 'fsdp'), 'tensor')
- qkv_bias: float32 [6144], P('tensor'), may hold values from -0.6 to 0.6
- proj_weight: bfloat16 [2048, 2048], P(('seq', 'fsdp'), 'tensor'), may hold values from -1.5 to 1.5
- proj_bias: float32 [2048], P('tensor'), may hold values from -3 to 3
- up_weight: bfloat16 [2048, 8192], P(('seq', 'fsdp'), 'tensor'), may hold values from -0.125 to 0.125
- up_bias: float32 [8192], P('tensor'), may hold values from -3 to 3
- down_weight: bfloat16 [2048, 8192], P(('seq', 'fsdp'), 'tensor'), may hold values from -0.0625 to 0.0625
- down_bias: float32 [2048], P('tensor'), may hold values from -3 to 3
Outputs:
- hidden_out: bfloat16 [2048, 2048], P(('seq', 'fsdp'), 'tensor')
- input_grad: bfloat16 [2048, 2048], P(('seq', 'fsdp'), 'tensor')
- attn_gain_grad: float32 [2048], replicated
- attn_bias_grad: float32 [2048], replicated
- mlp_gain_grad: float32 [2048], replicated
- mlp_bias_grad: float32 [2048], replicated
- qkv_weight_grad: float32 [2048, 6144], P(('seq', 'fsdp'), 'tensor')
- qkv_bias_grad: float32 [6144], P('tensor')
- proj_weight_grad: float32 [2048, 2048], P(('seq', 'fsdp'), 'tensor')
- proj_bias_grad: float32 [2048], P('tensor')
- up_weight_grad: float32 [2048, 8192], P(('seq', 'fsdp'), 'tensor')
- up_bias_grad: float32 [8192], P('tensor')
- down_weight_grad: float32 [2048, 8192], P(('seq', 'fsdp'), 'tensor')
- down_bias_grad: float32 [2048], P('tensor')
All inputs are finite; a program needn't handle non-finite values.
Results may differ from a plain program's by a relative error of at most 0.013.
Values may be sent and summed in bfloat16 or wider, within the bound.
A program may use at most 256 MiB of HBM per device.

v0:
```python
import functools
import math

import jax
import jax.numpy as jnp
import numpy as np
from jax import lax
from jax.experimental import pallas as pl
from jax.experimental.pallas import tpu as pltpu
from jax.sharding import PartitionSpec as P

HEAD_DIM = 256
ROT = 64
LANES = 128
STRIP = 256
MESH = pl.DeviceIdType.MESH
VMEM_BYTES = 63 << 20

norm_eps = 1e-05
rope_base = 10000.0


def bits_of(size):
    return [1 << b for b in range(size.bit_length() - 1)]


def bf(value):
    return value.astype(jnp.bfloat16)


def f32(value):
    return value.astype(jnp.float32)


def mm(left, right, left_dim, right_dim):
    return lax.dot_general(
        left, right, (((left_dim,), (right_dim,)), ((), ())), preferred_element_type=jnp.float32
    )


def rotary_tables(tok, blocks):
    half = ROT // 2
    frequency = rope_base ** (-np.arange(half, dtype=np.float64) * 2.0 / ROT)
    lanes = np.zeros(LANES)
    lanes[:half] = frequency
    lanes[half:ROT] = frequency
    inner = np.arange(tok, dtype=np.float64)[:, None] * lanes
    outer = np.arange(blocks, dtype=np.float64)[:, None] * tok * lanes
    pack = lambda a: np.stack([np.cos(a), np.sin(a)]).astype(np.float32)
    return (jnp.asarray(pack(inner)), jnp.asarray(pack(outer)))


def flip(rank, mask, size):
    out = jnp.int32(0)
    for b in range(size.bit_length() - 1):
        digit = lax.rem(lax.div(rank, jnp.int32(1 << b)), jnp.int32(2))
        out = out + ((1 - digit) if mask >> b & 1 else digit) * (1 << b)
    return out


def low_bit(j, size):
    return j & -j if j else size


def line_mask(j):
    mask = 0
    b = 0
    while j >> b:
        if j >> b & 1:
            mask ^= (2 << b) - 1
        b += 1
    return mask


def arrivals(size):
    return sorted(range(1, size), key=lambda j: (-low_bit(j, size), j))


def slot_of(j, bit, size):
    index = 0
    for jj in range(size):
        for bb in bits_of(size):
            if bb < low_bit(jj, size):
                if (jj, bb) == (j, bit):
                    return index
                index += 1
    raise ValueError


def at(index, size):
    return pl.ds(pl.multiple_of(index * size, size), size)


def greet(S, T, F, z, y, f):
    barrier = pltpu.get_barrier_semaphore()
    peers = [{"seq": flip(z, k, S)} for k in range(1, S)]
    peers += [{"tensor": flip(y, t, T)} for t in range(1, T)]
    peers += [{"fsdp": flip(f, b, F)} for b in bits_of(F)]
    for peer in peers:
        pl.semaphore_signal(barrier, inc=1, device_id=peer, device_id_type=MESH)
    pl.semaphore_wait(barrier, len(peers))


def remote(src, dst, send, recv, peer):
    return pltpu.make_async_remote_copy(
        src_ref=src, dst_ref=dst, send_sem=send, recv_sem=recv, device_id=peer, device_id_type=MESH
    )


def repeat(count, body):
    def step(i, carry):
        body(i)
        return carry

    lax.fori_loop(0, count, step, 0)


def turn(value, cos_part, sin_part):
    half = ROT // 2
    head = value[:, :LANES]
    lane = lax.broadcasted_iota(jnp.int32, head.shape, 1)
    other = jnp.where(
        lane < half, -pltpu.roll(head, LANES - half, 1), pltpu.roll(head, half, 1)
    )
    return jnp.concatenate([head * cos_part + other * sin_part, value[:, LANES:]], axis=1)


def first_kernel(S, T, F, *refs):
    hid_in, cot_in, wq_in, wp_in, wu_in, wd_in = refs[:6]
    attn_gain, attn_bias, mlp_gain, mlp_bias, qkv_bias, up_bias, inner, outer = refs[6:14]
    hid_o, cot_o, attn_in_o, mlp_in_o, stat_o, wq_o, wp_o, wu_o, wd_o = refs[14:23]
    attn_o, active_o, slope_o, tg_o = refs[23:27]
    hid, cot, attn_in, mlp_in, stat, wq, wp, wu, wd = refs[27:36]
    attn, active, slope, tg = refs[36:40]
    query, pair, attn_grad, probs, score_grad, row_info, part_in = refs[40:47]
    own_sem, out_sem, tok_send, tok_recv, row_send, row_recv = refs[47:53]
    pair_send, pair_recv, part_send, part_recv = refs[53:57]
    z, y, f = lax.axis_index("seq"), lax.axis_index("tensor"), lax.axis_index("fsdp")
    fbits = bits_of(F)
    tok, width = hid_in.shape
    ntok, D = hid.shape
    rows = wq_in.shape[0]
    keys = pair.shape[0]
    scale = HEAD_DIM ** (-0.5)
    tokens = ((hid_in, hid), (cot_in, cot))
    weights = ((wq_in, wq), (wp_in, wp), (wu_in, wu), (wd_in, wd))
    sends, pair_sends = [], []

    def start(copy):
        copy.start()
        sends.append(copy)

    def tok_sem(a, j, t):
        return (a * S + j) * T + t

    def tok_place(a, j, t):
        return tokens[a][1].at[at(flip(z, line_mask(j), S), tok), at(flip(y, t, T), width)]

    def tok_forward(a, j):
        src = tokens[a][0] if j == 0 else tok_place(a, j, 0)
        dst = tok_place(a, j, 0)
        for b in reversed(bits_of(S)):
            if b < low_bit(j, S):
                i = tok_sem(a, j + b, 0)
                peer = {"seq": flip(z, line_mask(b), S)}
                start(remote(src, dst, tok_send.at[i], tok_recv.at[i], peer))
        for t in range(1, T):
            i = tok_sem(a, j, t)
            peer = {"tensor": flip(y, t, T)}
            start(remote(src, dst, tok_send.at[i], tok_recv.at[i], peer))

    def tok_wait(a, j, t):
        i = tok_sem(a, j, t)
        spot = tok_place(a, j, t)
        remote(spot, spot, tok_send.at[i], tok_recv.at[i], {"tensor": flip(y, 1, T)}).wait_recv()

    def tok_seq(a):
        for j in arrivals(S):
            tok_wait(a, j, 0)
            tok_forward(a, j)

    def tok_rest(a):
        tok_own(a).wait()
        for j in range(S):
            for t in range(1, T):
                tok_wait(a, j, t)

    def tok_own(a):
        return pltpu.make_async_copy(tokens[a][0], tok_place(a, 0, 0), own_sem.at[a])

    def row_sem(m, k, j):
        return (m * S + k) * F + j

    def row_place(m, k, j):
        return weights[m][1].at[at(flip(z, k, S) * F + flip(f, j, F), rows), :]

    def row_source(m, zd):
        src, dst = weights[m]
        return src.at[:, at(zd, dst.shape[1])]

    def row_seq(m):
        for k in range(1, S):
            i = row_sem(m, k, 0)
            zd = flip(z, k, S)
            start(
                remote(
                    row_source(m, zd), row_place(m, 0, 0), row_send.at[i], row_recv.at[i], {"seq": zd}
                )
            )

    def row_forward(m, k, j):
        dst = row_place(m, k, j)
        src = row_source(m, z) if k == 0 and j == 0 else dst
        for b in reversed(fbits):
            if b < low_bit(j, F):
                i = row_sem(m, k, j + b)
                peer = {"fsdp": flip(f, b, F)}
                start(remote(src, dst, row_send.at[i], row_recv.at[i], peer))

    def row_wait(m, k, j):
        i = row_sem(m, k, j)
        spot = row_place(m, k, j)
        remote(spot, spot, row_send.at[i], row_recv.at[i], {"seq": flip(z, 1, S)}).wait_recv()

    def row_own(m):
        return pltpu.make_async_copy(row_source(m, z), row_place(m, 0, 0), own_sem.at[2 + m])

    def row_arrive(m):
        for k in range(1, S):
            row_wait(m, k, 0)
            row_forward(m, k, 0)

    def row_relay(m):
        for j in arrivals(F):
            if low_bit(j, F) > 1:
                for k in range(S):
                    row_wait(m, k, j)
                    row_forward(m, k, j)

    def row_rest(m):
        row_own(m).wait()
        for j in arrivals(F):
            if low_bit(j, F) == 1:
                for k in range(S):
                    row_wait(m, k, j)

    def pair_place(zd, j):
        return pair.at[at(zd * F + flip(f, j, F), tok), :]

    def pair_forward(zd, j):
        spot = pair_place(zd, j)
        for b in reversed(fbits):
            if b < low_bit(j, F):
                i = zd * F + j + b
                peer = {"fsdp": flip(f, b, F)}
                copy = remote(spot, spot, pair_send.at[i], pair_recv.at[i], peer)
                copy.start()
                pair_sends.append(copy)

    def pair_wait(zd, j):
        i = zd * F + j
        spot = pair_place(zd, j)
        remote(spot, spot, pair_send.at[i], pair_recv.at[i], {"fsdp": flip(f, 1, F)}).wait_recv()

    outs = []

    def put(src, dst):
        copy = pltpu.make_async_copy(src, dst, out_sem.at[len(outs)])
        copy.start()
        outs.append(copy)

    greet(S, T, F, z, y, f)
    tok_forward(0, 0)
    tok_own(0).start()
    row_seq(0)
    row_forward(0, 0, 0)
    row_own(0).start()
    tok_forward(1, 0)
    tok_own(1).start()
    for m in range(1, 4):
        row_seq(m)
        row_forward(m, 0, 0)
        row_own(m).start()

    tok_seq(0)
    tok_rest(0)
    put(hid, hid_o)
    chunk = 32

    def norm_chunk(i):
        part = at(i, chunk)
        x = f32(hid[part, :])
        mean = jnp.mean(x, axis=-1, keepdims=True)
        centered = x - mean
        inv_std = lax.rsqrt(jnp.mean(centered * centered, axis=-1, keepdims=True) + norm_eps)
        xhat = centered * inv_std
        attn_in[part, :] = bf(xhat * attn_gain[...] + attn_bias[...])
        mlp_in[part, :] = bf(xhat * mlp_gain[...] + mlp_bias[...])
        stat[0, part, :] = jnp.broadcast_to(mean, (chunk, LANES))
        stat[1, part, :] = jnp.broadcast_to(inv_std, (chunk, LANES))

    repeat(ntok // chunk, norm_chunk)
    put(attn_in, attn_in_o)
    put(mlp_in, mlp_in_o)
    put(stat, stat_o)

    def angles(zd, here=slice(None)):
        block = pl.ds(zd * F + f, 1)
        cos_in, sin_in = inner[0, here, :], inner[1, here, :]
        cos_out, sin_out = outer[0, block, :], outer[1, block, :]
        return (cos_in * cos_out - sin_in * sin_out, sin_in * cos_out + cos_in * sin_out)

    row_arrive(0)
    row_relay(0)
    row_rest(0)
    put(wq, wq_o)
    bias = qkv_bias[:, at(z, 3 * HEAD_DIM)]
    for c in range(3):
        part = mm(attn_in[...], wq[:, c * HEAD_DIM : (c + 1) * HEAD_DIM], 1, 0)
        part = part + bias[:, c * HEAD_DIM : (c + 1) * HEAD_DIM]
        for zd in range(S):
            piece = part[zd * tok : (zd + 1) * tok]
            if c < 2:
                piece = turn(piece, *angles(zd))
            if c == 0:
                query[zd * tok : (zd + 1) * tok, :] = bf(piece)
            else:
                spot = at(zd * F + f, tok)
                pair[spot, (c - 1) * HEAD_DIM : c * HEAD_DIM] = bf(piece)
    for zd in range(S):
        pair_forward(zd, 0)

    tok_seq(1)
    row_arrive(1)
    for j in arrivals(F):
        for zd in range(S):
            pair_wait(zd, j)
            pair_forward(zd, j)
    row_relay(1)

    qc = max(32, min(tok, tok * 2048 // keys))

    def masked_scores(zd, i, n):
        start_row = zd * tok + i * qc
        q = query[pl.ds(pl.multiple_of(start_row, qc), qc), :]
        scores = mm(q, pair[:n, :HEAD_DIM], 1, 1) * scale
        last = (zd * F + f) * tok + i * qc
        ahead = lax.broadcasted_iota(jnp.int32, scores.shape, 1) - lax.broadcasted_iota(
            jnp.int32, scores.shape, 0
        )
        return (scores, ahead <= last)

    for zd in range(S):
        n = (zd + 1) * F * tok

        def forward_chunk(i, zd=zd, n=n):
            here = pl.ds(pl.multiple_of(zd * tok + i * qc, qc), qc)
            scores, allowed = masked_scores(zd, i, n)
            top = jnp.max(jnp.where(allowed, scores, -1e30), axis=-1, keepdims=True)
            terms = jnp.where(allowed, jnp.exp(scores - top), 0.0)
            total = jnp.sum(terms, axis=-1, keepdims=True)
            mixed = mm(bf(terms), pair[:n, HEAD_DIM:], 1, 0) / total
            attn[here, :] = bf(mixed)
            row_info[here, :] = jnp.broadcast_to(top + jnp.log(total), (qc, LANES))

        repeat(tok // qc, forward_chunk)
    put(attn, attn_o)

    tok_rest(1)
    put(cot, cot_o)
    row_rest(1)
    put(wp, wp_o)
    attn_grad[...] = bf(mm(cot[...], wp[...], 1, 0))
    row_arrive(2)
    row_relay(2)
    for zd in range(S):
        n = (zd + 1) * F * tok

        def backward_chunk(i, zd=zd, n=n):
            here = pl.ds(pl.multiple_of(zd * tok + i * qc, qc), qc)
            scores, allowed = masked_scores(zd, i, n)
            weights_here = jnp.where(allowed, jnp.exp(scores - row_info[here, :1]), 0.0)
            grad = attn_grad[here, :]
            delta = jnp.sum(f32(grad) * f32(attn[here, :]), axis=-1, keepdims=True)
            slopes = mm(grad, pair[:n, HEAD_DIM:], 1, 1)
            inner_grad = bf(weights_here * (slopes - delta))
            probs[here, :n] = bf(weights_here)
            score_grad[here, :n] = inner_grad
            if n < keys:
                blank = jnp.zeros((qc, keys - n), jnp.bfloat16)
                probs[here, n:] = blank
                score_grad[here, n:] = blank
            cos_part, sin_part = angles(zd, pl.ds(pl.multiple_of(i * qc, qc), qc))
            grad_here = mm(inner_grad, pair[:n, :HEAD_DIM], 1, 0) * scale
            tg[here, :HEAD_DIM] = bf(turn(grad_here, cos_part, -sin_part))

        repeat(tok // qc, backward_chunk)

    def part_sum(j):
        def lanes(ref):
            return jnp.concatenate(
                [ref[:, at(zd * F + flip(f, j, F), tok)] for zd in range(S)], axis=1
            )

        total = jnp.concatenate(
            [mm(lanes(score_grad), query[...], 0, 0) * scale, mm(lanes(probs), attn_grad[...], 0, 0)],
            axis=1,
        )
        for b in fbits:
            if b < low_bit(j, F):
                i = slot_of(j, b, F)
                spot = part_in.at[i]
                peer = {"fsdp": flip(f, b, F)}
                remote(spot, spot, part_send.at[i], part_recv.at[i], peer).wait_recv()
                total = total + f32(part_in[i])
        return total

    for copy in pair_sends:
        copy.wait_send()

    def part_stage(bit):
        for j in range(1, F):
            if low_bit(j, F) == bit:
                spot = pair.at[(j - 1) * ntok : j * ntok, :]
                pair[(j - 1) * ntok : j * ntok, :] = bf(part_sum(j))
                i = slot_of(j - bit, bit, F)
                peer = {"fsdp": flip(f, bit, F)}
                start(remote(spot, part_in.at[i], part_send.at[j - 1], part_recv.at[i], peer))

    part_stage(fbits[0])
    row_rest(2)
    put(wu, wu_o)

    cols = wu.shape[1]
    for n in range(cols // STRIP):
        strip = slice(n * STRIP, (n + 1) * STRIP)
        mid = mm(mlp_in[...], wu[:, strip], 1, 0) + up_bias[
            :, pl.ds(pl.multiple_of(z * cols + n * STRIP, STRIP), STRIP)
        ]
        cdf = 0.5 * (1.0 + lax.erf(mid * 0.7071067811865476))
        active[:, strip] = bf(mid * cdf)
        slope[:, strip] = cdf + mid * jnp.exp(-0.5 * mid * mid) * 0.3989422804014327
        if n == 0:
            for bit in fbits[1:]:
                part_stage(bit)
    put(active, active_o)
    put(slope, slope_o)
    row_arrive(3)
    total = part_sum(0)
    for zd in range(S):
        here = slice(zd * tok, (zd + 1) * tok)
        cos_part, sin_part = angles(zd)
        tg[here, HEAD_DIM : 2 * HEAD_DIM] = bf(turn(total[here, :HEAD_DIM], cos_part, -sin_part))
        tg[here, 2 * HEAD_DIM :] = bf(total[here, HEAD_DIM:])
    put(tg, tg_o)
    row_relay(3)
    row_rest(3)
    put(wd, wd_o)
    for copy in outs:
        copy.wait()
    for copy in sends:
        copy.wait_send()


def first_call(S, T, F, arrays, vectors):
    hidden, _, wq, wp, wu, _ = arrays
    tok, width = hidden.shape
    rows = wq.shape[0]
    ntok, D, keys = S * tok, T * width, S * F * tok
    if width != S * HEAD_DIM or S * F * rows != D:
        raise ValueError
    small, wide = jnp.bfloat16, jnp.float32
    ff = wu.shape[1] // S
    inner, outer = rotary_tables(tok, S * F)
    outs = [((ntok, D), small)] * 4 + [((2, ntok, LANES), wide)]
    outs += [((D, w.shape[1] // S), small) for w in arrays[2:]]
    outs += [((ntok, HEAD_DIM), small), ((ntok, ff), small), ((ntok, ff), wide)]
    outs += [((ntok, 3 * HEAD_DIM), small)]
    n_part = max(F - 1, 1)
    scratch = outs + [
        ((ntok, HEAD_DIM), small),
        ((keys, 2 * HEAD_DIM), small),
        ((ntok, HEAD_DIM), small),
        ((ntok, keys), small),
        ((ntok, keys), small),
        ((ntok, LANES), wide),
        ((n_part, ntok, 2 * HEAD_DIM), small),
    ]
    dma = pltpu.SemaphoreType.DMA
    any_spec = pl.BlockSpec(memory_space=pl.ANY)
    vmem = pl.BlockSpec(memory_space=pltpu.VMEM)
    return pl.pallas_call(
        functools.partial(first_kernel, S, T, F),
        out_shape=[jax.ShapeDtypeStruct(*o) for o in outs],
        in_specs=[any_spec] * 6 + [vmem] * 8,
        out_specs=[any_spec] * len(outs),
        scratch_shapes=[pltpu.VMEM(*o) for o in scratch]
        + [
            dma((6,)),
            dma((len(outs),)),
            dma((2 * S * T,)),
            dma((2 * S * T,)),
            dma((4 * S * F,)),
            dma((4 * S * F,)),
            dma((S * F,)),
            dma((S * F,)),
            dma((n_part,)),
            dma((n_part,)),
        ],
        compiler_params=pltpu.CompilerParams(
            collective_id=0, has_side_effects=True, vmem_limit_bytes=VMEM_BYTES
        ),
    )(*arrays, *vectors, inner, outer)


def second_kernel(S, T, F, turned, *refs):
    cot_i, hid_i, attn_in_i, mlp_in_i, stat_i, wq_i, wp_i, wu_i, wd_i = refs[:9]
    attn_i, active_i, slope_i, tg_i, own_cot, attn_gain, mlp_gain = refs[9:16]
    grads, refs = refs[16:20], refs[20:]
    homes, (gain_o, qkv_bias_o, up_bias_o, out_bias_o), refs = refs[:2], refs[2:6], refs[6:]
    cot, hid, attn_in, mlp_in, stat, wq, wp, wud, attn, active, tg, pre = refs[:12]
    wide, own_half, sums, vec, vec_in, vec_seq, vec_ten = refs[12:19]
    out_b, in_b, seq_b, refs = refs[19:23], refs[23:27], refs[27:31], refs[31:]
    y_out, y_in, z_out, z_in, home_v = refs[:5]
    load_sem, own_sem, out_sem, in_sem, seq_send, seq_recv = refs[5:11]
    y_send, y_recv, z_send, z_recv, v_send, v_recv = refs[11:17]
    z, y, f = lax.axis_index("seq"), lax.axis_index("tensor"), lax.axis_index("fsdp")
    fbits, sbits = bits_of(F), bits_of(S)
    tok, width = homes[0].shape
    ntok, D = wide.shape
    ff = active.shape[1]
    units = (
        (attn, cot, HEAD_DIM),
        (active, cot, ff),
        (tg, attn_in, 3 * HEAD_DIM),
        (pre, mlp_in, ff),
    )
    sends = []

    def start(copy):
        copy.start()
        sends.append(copy)

    loads = {}

    def load(name, src, dst):
        loads[name] = pltpu.make_async_copy(src, dst, load_sem.at[len(loads)])
        loads[name].start()

    waited = set()

    def need(*names):
        for name in names:
            if name not in waited:
                waited.add(name)
                loads[name].wait()

    load("cot", cot_i, cot)
    load("attn", attn_i, attn)
    load("active", active_i, active)
    load("wd", wd_i, wud)
    load("wp", wp_i, wp)
    load("slope", slope_i, wide.at[:, :ff])
    load("tg", tg_i, tg)
    load("attn_in", attn_in_i, attn_in)
    load("wq", wq_i, wq)
    load("hid", hid_i, hid)
    load("stat", stat_i, stat)
    load("mlp_in", mlp_in_i, mlp_in)

    greet(S, T, F, z, y, f)

    def block_sum(u, j):
        right, left, _ = units[u]
        rows = grads[u].shape[0]
        fd = flip(f, j, F)
        if turned:
            block = jnp.concatenate([left[at(zd * F + fd, rows), :] for zd in range(S)], axis=0)
            total = mm(block, right[...], 1, 0)
        else:
            block = jnp.concatenate([left[:, at(zd * F + fd, rows)] for zd in range(S)], axis=1)
            total = mm(block, right[...], 0, 0)
        for bit in fbits:
            if bit < low_bit(j, F):
                s = slot_of(j, bit, F)
                i = u * (F - 1) + s
                spot = in_b[u].at[s]
                peer = {"fsdp": flip(f, bit, F)}
                remote(spot, spot, out_sem.at[i], in_sem.at[i], peer).wait_recv()
                total = total + f32(in_b[u][s])
        return total

    def fsdp_stage(u, bit):
        for j in range(1, F):
            if low_bit(j, F) == bit:
                out_b[u][j - 1] = bf(block_sum(u, j))
                there = slot_of(j - bit, bit, F)
                start(
                    remote(
                        out_b[u].at[j - 1],
                        in_b[u].at[there],
                        out_sem.at[u * (F - 1) + j - 1],
                        in_sem.at[u * (F - 1) + there],
                        {"fsdp": flip(f, bit, F)},
                    )
                )

    def own_grad(u):
        rows = grads[u].shape[0]
        cols = units[u][2]
        return pltpu.make_async_copy(
            seq_b[u].at[at(z, rows), :], grads[u].at[:, at(z, cols)], own_sem.at[u]
        )

    def seq_stage(u):
        rows = grads[u].shape[0]
        cols = units[u][2]
        seq_b[u][...] = bf(block_sum(u, 0))
        for k in range(1, S):
            peer = flip(z, k, S)
            start(
                remote(
                    seq_b[u].at[at(peer, rows), :],
                    grads[u].at[:, at(z, cols)],
                    seq_send.at[u * S + k],
                    seq_recv.at[u * S + k],
                    {"seq": peer},
                )
            )
        own_grad(u).start()

    def seq_wait(u):
        cols = units[u][2]
        for k in range(1, S):
            spot = grads[u].at[:, at(flip(z, k, S), cols)]
            i = u * S + k
            remote(spot, spot, seq_send.at[i], seq_recv.at[i], {"seq": flip(z, k, S)}).wait_recv()
        own_grad(u).wait()

    def y_index(s, t, zd):
        return (s * max(T - 1, 1) + t - 1) * S + zd

    def y_store(s, t, column, value):
        for zd in range(S):
            y_out[y_index(s, t, zd), :, column] = bf(value[zd * tok : (zd + 1) * tok])

    def tensor_send(s):
        for j in [*sorted(range(1, S), key=lambda j: (low_bit(j, S), j)), 0]:
            zd = flip(z, line_mask(j), S)
            for t in range(1, T):
                i = y_index(s, t, 0) + j
                peer = {"tensor": flip(y, t, T)}
                here = y_out.at[y_index(s, t, zd)]
                start(remote(here, y_in.at[i], y_send.at[i], y_recv.at[i], peer))

    def token_part(s, j):
        zd = flip(z, line_mask(j), S)
        total = own_half[at(zd, tok), :]
        for t in range(1, T):
            i = y_index(s, t, 0) + j
            spot = y_in.at[i]
            remote(spot, spot, y_send.at[i], y_recv.at[i], {"tensor": flip(y, t, T)}).wait_recv()
            total = total + f32(y_in[i])
        for bit in sbits:
            if bit < low_bit(j, S):
                i = s * (S - 1) + slot_of(j, bit, S)
                spot = z_in.at[i]
                peer = {"seq": flip(z, line_mask(bit), S)}
                remote(spot, spot, z_send.at[i], z_recv.at[i], peer).wait_recv()
                total = total + f32(z_in[i])
        return total

    def token_stage(s, bit):
        for j in range(1, S):
            if low_bit(j, S) == bit:
                i = s * (S - 1) + j - 1
                there = s * (S - 1) + slot_of(j - bit, bit, S)
                z_out[i] = bf(token_part(s, j))
                peer = {"seq": flip(z, line_mask(bit), S)}
                start(remote(z_out.at[i], z_in.at[there], z_send.at[i], z_recv.at[there], peer))

    def home_copy(s):
        return pltpu.make_async_copy(home_v.at[s], homes[s], own_sem.at[4 + s])

    def token_home(s):
        home_v[s] = token_part(s, 0)
        home_copy(s).start()

    def vec_exchange(i, dst, peer):
        return remote(vec.at[i], dst, v_send.at[i], v_recv.at[i], peer)

    n_fsdp = len(fbits)

    def vec_fsdp(b):
        start(vec_exchange(b, vec_in.at[b], {"fsdp": flip(f, fbits[b], F)}))

    def vec_fsdp_sum(b):
        vec_exchange(b, vec_in.at[b], {"fsdp": flip(f, fbits[b], F)}).wait_recv()
        vec[b + 1] = vec[b] + vec_in[b]

    def vec_seq_copy(k):
        peer = {"seq": flip(z, k, S)}
        i = n_fsdp + k - 1
        return remote(vec.at[n_fsdp], vec_seq.at[k - 1], v_send.at[i], v_recv.at[i], peer)

    def vec_seq_sum():
        qkv_bias_o[:, at(z, 3 * HEAD_DIM)] = vec[n_fsdp, 4:5, : 3 * HEAD_DIM]
        up_bias_o[:, at(z, ff)] = vec[n_fsdp, 5:6, :ff]
        parts = [vec[n_fsdp]]
        for k in range(1, S):
            vec_seq_copy(k).wait_recv()
            zd = flip(z, k, S)
            qkv_bias_o[:, at(zd, 3 * HEAD_DIM)] = vec_seq[k - 1, 4:5, : 3 * HEAD_DIM]
            up_bias_o[:, at(zd, ff)] = vec_seq[k - 1, 5:6, :ff]
            parts.append(vec_seq[k - 1])
        while len(parts) > 1:
            parts = [a + b for a, b in zip(parts[::2], parts[1::2])]
        out_bias_o[...] = parts[0][6:7, :width]
        vec_ten[0] = parts[0][:4]

    def vec_ten_copy(t):
        peer = {"tensor": flip(y, t, T)}
        i = n_fsdp + S - 1 + t - 1
        return remote(vec_ten.at[0], vec_ten.at[t], v_send.at[i], v_recv.at[i], peer)

    def vec_ten_sum():
        parts = [vec_ten[0]]
        for t in range(1, T):
            vec_ten_copy(t).wait_recv()
            parts.append(vec_ten[t])
        while len(parts) > 1:
            parts = [a + b for a, b in zip(parts[::2], parts[1::2])]
        gain_o[...] = parts[0]

    need("cot", "attn")
    vec[0] = jnp.zeros(vec.shape[1:], jnp.float32)
    fsdp_stage(0, fbits[0])
    need("active", "wd", "wp")

    def branch(column):
        return mm(active[...], wud[column, :], 1, 1) + mm(attn[...], wp[column, :], 1, 1)

    for t in [*range(1, T), 0]:
        for n in range(width // STRIP):
            there = pl.ds(
                pl.multiple_of(flip(y, t, T) * width + n * STRIP, STRIP), STRIP
            )
            here = slice(n * STRIP, (n + 1) * STRIP)
            if t:
                y_store(0, t, here, branch(there))
            else:
                own_half[:, here] = branch(there)
        if t == T - 1:
            tensor_send(0)
    for bit in fbits[1:]:
        fsdp_stage(0, bit)
    fsdp_stage(1, fbits[0])
    seq_stage(0)
    token_stage(0, sbits[0])

    need("slope")
    for n in range(ff // STRIP):
        here = slice(n * STRIP, (n + 1) * STRIP)
        value = mm(cot[...], wud[:, here], 0 if turned else 1, 0) * wide[:, here]
        vec[0, 5:6, here] = jnp.sum(value, axis=0, keepdims=True)
        pre[:, here] = bf(value)
    load("wu", wu_i, wud)
    for bit in fbits[1:]:
        fsdp_stage(1, bit)
    for bit in sbits[1:]:
        token_stage(0, bit)
    need("tg", "attn_in")
    fsdp_stage(2, fbits[0])
    seq_stage(1)
    need("mlp_in")
    fsdp_stage(3, fbits[0])
    token_home(0)

    need("wu", "wq", "hid", "stat")
    lane_parts = range(0, STRIP, LANES)

    def norm_strip(n):
        here = at(n, STRIP)
        a = mm(tg[...], wq[here, :], 1, 1)
        m = mm(pre[...], wud[here, :], 1, 1)
        mean, inv_std = stat[0, :, :1], stat[1, :, :1]
        xhat = (f32(hid[:, here]) - mean) * inv_std
        vec[0, 0:1, here] = jnp.sum(a * xhat, axis=0, keepdims=True)
        vec[0, 1:2, here] = jnp.sum(a, axis=0, keepdims=True)
        vec[0, 2:3, here] = jnp.sum(m * xhat, axis=0, keepdims=True)
        vec[0, 3:4, here] = jnp.sum(m, axis=0, keepdims=True)
        both = a * attn_gain[:, here] + m * mlp_gain[:, here]
        wide[:, here] = both
        scaled = both * xhat
        sums[0] += sum(both[:, c : c + LANES] for c in lane_parts)
        sums[1] += sum(scaled[:, c : c + LANES] for c in lane_parts)

    sums[...] = jnp.zeros_like(sums)
    repeat(D // STRIP, norm_strip)
    vec[0, 4:5, : 3 * HEAD_DIM] = jnp.sum(f32(tg[...]), axis=0, keepdims=True)
    vec[0, 6:7, :width] = jnp.sum(f32(own_cot[...]), axis=0, keepdims=True)
    vec_fsdp(0)
    for bit in fbits[1:]:
        fsdp_stage(2, bit)
    sums[0] = jnp.broadcast_to(jnp.sum(sums[0], axis=-1, keepdims=True) / D, sums.shape[1:])
    sums[1] = jnp.broadcast_to(jnp.sum(sums[1], axis=-1, keepdims=True) / D, sums.shape[1:])

    def input_term(column):
        mean, inv_std = stat[0, :, :1], stat[1, :, :1]
        xhat = (f32(hid[:, column]) - mean) * inv_std
        return inv_std * (wide[:, column] - sums[0, :, :1] - xhat * sums[1, :, :1])

    for t in [*range(1, T), 0]:
        for n in range(width // STRIP):
            there = pl.ds(
                pl.multiple_of(flip(y, t, T) * width + n * STRIP, STRIP), STRIP
            )
            here = slice(n * STRIP, (n + 1) * STRIP)
            if t:
                y_store(1, t, here, input_term(there))
            else:
                own_half[:, here] = input_term(there)
        if t == T - 1:
            tensor_send(1)
    vec_fsdp_sum(0)
    for b in range(1, n_fsdp):
        vec_fsdp(b)
        if b == 1:
            seq_stage(2)
            for bit in fbits[1:]:
                fsdp_stage(3, bit)
        vec_fsdp_sum(b)
    for k in range(1, S):
        start(vec_seq_copy(k))
    token_stage(1, sbits[0])
    seq_stage(3)
    vec_seq_sum()
    for t in range(1, T):
        start(vec_ten_copy(t))
    for bit in sbits[1:]:
        token_stage(1, bit)
    vec_ten_sum()
    token_home(1)
    for u in range(4):
        seq_wait(u)
    for s in range(2):
        home_copy(s).wait()
    for copy in sends:
        copy.wait_send()


def second_call(S, T, F, first, own_cot, attn_gain, mlp_gain, rows):
    hid, cot, attn_in, mlp_in, stat, wq, wp, wu, wd, attn, active, slope, tg = first
    turned = rows % LANES != 0
    if turned:
        cot, attn_in, mlp_in = cot.T, attn_in.T, mlp_in.T
    tok, width = own_cot.shape
    ntok, D = hid.shape
    ff = active.shape[1]
    small, wide = jnp.bfloat16, jnp.float32
    cols = (HEAD_DIM, ff, 3 * HEAD_DIM, ff)
    parts, block, n_f = max(F - 1, 1), S * rows, F.bit_length() - 1
    ins = (cot, hid, attn_in, mlp_in, stat, wq, wp, wu, wd, attn, active, slope, tg)
    any_spec = pl.BlockSpec(memory_space=pl.ANY)
    vmem = pl.BlockSpec(memory_space=pltpu.VMEM)
    dma = pltpu.SemaphoreType.DMA
    shape = jax.ShapeDtypeStruct
    scratch = [(a.shape, small) for a in (cot, hid, attn_in, mlp_in)] + [(stat.shape, wide)]
    scratch += [(a.shape, small) for a in (wq, wp, wu, attn, active, tg)]
    scratch += [
        ((ntok, ff), small),
        ((ntok, D), wide),
        ((ntok, width), wide),
        ((2, ntok, LANES), wide),
        ((n_f + 1, 8, D), wide),
        ((n_f, 8, D), wide),
        ((max(S - 1, 1), 8, D), wide),
        ((T, 4, D), wide),
    ]
    scratch += [((parts, block, c), small) for c in cols] * 2
    scratch += [((block, c), small) for c in cols]
    n_y, n_z, n_v = 2 * max(T - 1, 1) * S, 2 * max(S - 1, 1), n_f + S + T
    scratch += [((n_y, tok, width), small)] * 2 + [((n_z, tok, width), small)] * 2
    scratch += [((2, tok, width), wide)]
    return pl.pallas_call(
        functools.partial(second_kernel, S, T, F, turned),
        out_shape=[shape((rows, S * c), small) for c in cols]
        + [shape((tok, width), wide)] * 2
        + [shape((4, D), wide), shape((1, 3 * width), wide)]
        + [shape((1, S * ff), wide), shape((1, width), wide)],
        in_specs=[any_spec] * len(ins) + [vmem] * 3,
        out_specs=[any_spec] * 6 + [vmem] * 4,
        scratch_shapes=[pltpu.VMEM(*s) for s in scratch]
        + [
            dma((len(ins),)),
            dma((6,)),
            dma((4 * parts,)),
            dma((4 * parts,)),
            dma((4 * S,)),
            dma((4 * S,)),
            dma((n_y,)),
            dma((n_y,)),
            dma((n_z,)),
            dma((n_z,)),
            dma((n_v,)),
            dma((n_v,)),
        ],
        compiler_params=pltpu.CompilerParams(
            collective_id=1, has_side_effects=True, vmem_limit_bytes=VMEM_BYTES
        ),
    )(*ins, own_cot, attn_gain, mlp_gain)


def per_device(
    hidden_in,
    out_cotangent,
    attn_norm_gain,
    attn_norm_bias,
    mlp_norm_gain,
    mlp_norm_bias,
    qkv_weight,
    qkv_bias,
    proj_weight,
    proj_bias,
    up_weight,
    up_bias,
    down_weight,
    down_bias,
):
    sizes = [lax.axis_size(a) for a in ("seq", "tensor", "fsdp")]
    flat = [
        v.reshape(1, -1)
        for v in (attn_norm_gain, attn_norm_bias, mlp_norm_gain, mlp_norm_bias, qkv_bias, up_bias)
    ]
    first = first_call(
        *sizes,
        (hidden_in, out_cotangent, qkv_weight, proj_weight, up_weight, down_weight),
        flat,
    )
    proj, down, qkv, up, branch, norm, gains, qkv_bias_grad, up_bias_grad, out_bias_grad = (
        second_call(*sizes, first, out_cotangent, flat[0], flat[2], qkv_weight.shape[0])
    )
    hidden_out = bf(f32(hidden_in) + branch + proj_bias + down_bias)
    input_grad = bf(f32(out_cotangent) + norm)
    out_bias_grad = out_bias_grad.reshape(-1)
    return (
        hidden_out,
        input_grad,
        gains[0],
        gains[1],
        gains[2],
        gains[3],
        f32(qkv),
        qkv_bias_grad.reshape(-1),
        f32(proj),
        out_bias_grad,
        f32(up),
        up_bias_grad.reshape(-1),
        f32(down),
        out_bias_grad,
    )


def solution(mesh):
    matrix = P(("seq", "fsdp"), "tensor")
    vector = P("tensor")
    return jax.shard_map(
        per_device,
        mesh=mesh,
        in_specs=(
            matrix, matrix, P(), P(), P(), P(),
            matrix, vector, matrix, vector, matrix, vector, matrix, vector,
        ),
        out_specs=(
            matrix, matrix, P(), P(), P(), P(),
            matrix, vector, matrix, vector, matrix, vector, matrix, vector,
        ),
        check_vma=False,
    )
```

profile of v0, /device:TPU:8, one launch (start us, length us, event | category | flops | bytes accessed | tf_op | source)
XLA Modules:
  0.0 340.2 jit_solution(8863211341317379477)
XLA Ops:
  0.6 192.8 %shard_map.263 = (bf16[512,2048]{1,0:T(8,128)(2,1)}, bf16[512,2048]{1,0:T(8,128)(2,1)}, bf16[512,2048]{1,0:T(8,128)(2,1)}, bf16[512,2048]{1,0:T(8,128)(2,1)}, f3...) custom-call(bf16[128,1024]{1,0:T(8,128)(2,1)} %refs_0_.1, ...), custom_call_target="tpu_custom_call" | custom-call | tf_op jit(solution)/shard_map/pallas_call | solution.py:492
  193.5 0.0 copy-start
  193.5 0.0 copy-start.3
  193.5 0.0 copy-start.10
  193.5 0.0 copy-start.11
  193.5 136.1 %shard_map.264 = (bf16[128,1024]{1,0:T(8,128)(2,1)}, bf16[128,4096]{1,0:T(8,128)(2,1)}, bf16[128,3072]{1,0:T(8,128)(2,1)}, bf16[128,4096]{1,0:T(8,128)(2,1)}, f3...) custom-call(bf16[512,2048]{1,0:T(8,128)(2,1)} %get-tuple-element.37., ...), custom_call_target="tpu_custom_call" | custom-call | tf_op jit(solution)/shard_map/pallas_call | solution.py:885
  329.6 0.0 copy-start.6
  329.6 0.0 copy-start.5
  329.7 0.0 copy-start.4
  329.7 0.0 copy-done
  329.7 0.0 copy-done.3
  329.7 0.0 copy-done.10
  329.7 0.0 copy-done.11
  329.7 2.2 add_convert_fusion
  331.9 0.0 copy-start.2
  331.9 0.0 copy-done.6
  331.9 0.6 fusion
  332.6 0.0 copy-done.5
  332.6 0.8 convert_element_type.29
  333.4 0.0 copy-done.4
  333.4 1.3 convert_element_type.28
  334.7 0.0 copy-done.2
  334.7 0.0 copy-start.1
  334.7 1.5 convert_element_type.30
  336.2 0.0 copy-done.1
  336.2 0.0 copy-start.8
  336.2 0.0 copy-start.9
  336.2 0.0 copy-start.7
  336.3 1.5 convert_element_type.31
  337.8 0.0 copy-done.8
  337.8 0.6 copy.34
  338.4 0.0 copy-done.9
  338.4 0.6 copy.35
  339.0 0.6 copy.36
  339.6 0.0 copy-done.7
  339.6 0.6 copy.37
Async XLA Ops:
  193.5 136.2 %copy-start = (bf16[128,1024]{1,0:T(8,128)(2,1)S(1)}, bf16[128,1024]{1,0:T(8,128)(2,1)}, u32[]{:S(2)}) copy-start(bf16[128,1024]{1,0:T(8,128)(2,1)} %refs_13_.2) | copy-start | bytes 786436
  193.5 136.2 %copy-start.3 = (bf16[128,1024]{1,0:T(8,128)(2,1)S(1)}, bf16[128,1024]{1,0:T(8,128)(2,1)}, u32[]{:S(2)}) copy-start(bf16[128,1024]{1,0:T(8,128)(2,1)} %refs_0_.1) | copy-start | bytes 786436
  193.5 136.2 %copy-start.10 = (f32[1024]{0:T(1024)S(1)}, f32[1024]{0:T(1024)}, u32[]{:S(2)}) copy-start(f32[1024]{0:T(1024)} %param.29) | copy-start | bytes 12292
  193.5 136.2 %copy-start.11 = (f32[1024]{0:T(1024)S(1)}, f32[1024]{0:T(1024)}, u32[]{:S(2)}) copy-start(f32[1024]{0:T(1024)} %param.25) | copy-start | bytes 12292
  329.6 2.3 copy-start.6
  329.6 2.9 copy-start.5
  329.7 3.8 %copy-start.4 = (bf16[128,3072]{1,0:T(8,128)(2,1)S(1)}, bf16[128,3072]{1,0:T(8,128)(2,1)}, u32[]{:S(2)}) copy-start(bf16[128,3072]{1,0:T(8,128)(2,1)} %get-tuple-element.53) | copy-start | bytes 2359300
  331.9 2.8 copy-start.2
  334.7 1.5 copy-start.1
  336.2 1.5 copy-start.8
  336.2 2.1 copy-start.9
  336.2 3.3 copy-start.7
where the time goes:
time: 340 us
  Pallas kernels  329 us (97%)
  other arithmetic  7.42 us (2%)
    pallas_call x1, Pallas kernels, first_call(): pl.pallas_call(functools.partial(first_kernel, S, T, F), out_shape=[jax.S...  193 us
    pallas_call x1, Pallas kernels, second_call(): pl.pallas_call(functools.partial(second_kernel, S, T, F, turned), out_sha...  136 us

commit v1 on v0

--- a/solution.py
+++ b/solution.py
@@ -13,8 +13,9 @@
 ROT = 64
 LANES = 128
 STRIP = 256
+TOKEN_PARTS = 4
 MESH = pl.DeviceIdType.MESH
-VMEM_BYTES = 63 << 20
+VMEM_BYTES = 67_043_328
 
 norm_eps = 1e-05
 rope_base = 10000.0
@@ -129,12 +130,13 @@
     hid_in, cot_in, wq_in, wp_in, wu_in, wd_in = refs[:6]
     attn_gain, attn_bias, mlp_gain, mlp_bias, qkv_bias, up_bias, inner, outer = refs[6:14]
     hid_o, cot_o, attn_in_o, mlp_in_o, stat_o, wq_o, wp_o, wu_o, wd_o = refs[14:23]
-    attn_o, active_o, slope_o, tg_o = refs[23:27]
-    hid, cot, attn_in, mlp_in, stat, wq, wp, wu, wd = refs[27:36]
-    attn, active, slope, tg = refs[36:40]
-    query, pair, attn_grad, probs, score_grad, row_info, part_in = refs[40:47]
-    own_sem, out_sem, tok_send, tok_recv, row_send, row_recv = refs[47:53]
-    pair_send, pair_recv, part_send, part_recv = refs[53:57]
+    attn_o, active_o, slope_o, tg_o, proj_o = refs[23:28]
+    hid, cot, attn_in, mlp_in, stat, wq, wp, wu, wd = refs[28:37]
+    attn, active, slope, tg, proj = refs[37:42]
+    query, pair, attn_grad, probs, score_grad, row_info, part_in = refs[42:49]
+    proj_full, proj_out, proj_in = refs[49:52]
+    own_sem, out_sem, tok_send, tok_recv, row_send, row_recv = refs[52:58]
+    pair_send, pair_recv, part_send, part_recv, proj_send, proj_recv = refs[58:64]
     z, y, f = lax.axis_index("seq"), lax.axis_index("tensor"), lax.axis_index("fsdp")
     fbits = bits_of(F)
     tok, width = hid_in.shape
@@ -143,41 +145,72 @@
     keys = pair.shape[0]
     scale = HEAD_DIM ** (-0.5)
     tokens = ((hid_in, hid), (cot_in, cot))
-    weights = ((wq_in, wq), (wp_in, wp), (wu_in, wu), (wd_in, wd))
+    half = wu.shape[1] // 2
+    parts = TOKEN_PARTS
+    weights = (
+        (wq_in, wq, 0, wq.shape[1]),
+        (wp_in, wp, 0, wp.shape[1]),
+        (wu_in, wu, 0, half),
+        (wu_in, wu, half, half),
+        (wd_in, wd, 0, half),
+        (wd_in, wd, half, half),
+    )
     sends, pair_sends = [], []
 
     def start(copy):
         copy.start()
         sends.append(copy)
 
-    def tok_sem(a, j, t):
-        return (a * S + j) * T + t
+    def tok_sem(a, j, t, part):
+        return ((a * S + j) * T + t) * parts + part
 
     def tok_place(a, j, t):
         return tokens[a][1].at[at(flip(z, line_mask(j), S), tok), at(flip(y, t, T), width)]
 
-    def tok_forward(a, j):
+    def tok_split(j, t):
+        size = tok // parts if t == 0 else tok
+        return [(p, slice(p * size, (p + 1) * size)) for p in range(tok // size)]
+
+    def tok_seq(a, j):
         src = tokens[a][0] if j == 0 else tok_place(a, j, 0)
         dst = tok_place(a, j, 0)
         for b in reversed(bits_of(S)):
             if b < low_bit(j, S):
-                i = tok_sem(a, j + b, 0)
                 peer = {"seq": flip(z, line_mask(b), S)}
-                start(remote(src, dst, tok_send.at[i], tok_recv.at[i], peer))
+                for p, here in tok_split(j + b, 0):
+                    i = tok_sem(a, j + b, 0, p)
+                    start(remote(src.at[here], dst.at[here], tok_send.at[i], tok_recv.at[i], peer))
+
+    def tok_forward(a, j):
+        tok_seq(a, j)
+        tok_tensor(a, j)
+
+    def tok_tensor(a, j):
+        src = tokens[a][0] if j == 0 else tok_place(a, j, 0)
+        dst = tok_place(a, j, 0)
         for t in range(1, T):
-            i = tok_sem(a, j, t)
+            i = tok_sem(a, j, t, 0)
             peer = {"tensor": flip(y, t, T)}
             start(remote(src, dst, tok_send.at[i], tok_recv.at[i], peer))
 
     def tok_wait(a, j, t):
-        i = tok_sem(a, j, t)
         spot = tok_place(a, j, t)
-        remote(spot, spot, tok_send.at[i], tok_recv.at[i], {"tensor": flip(y, 1, T)}).wait_recv()
-
-    def tok_seq(a):
-        for j in arrivals(S):
+        for p, here in tok_split(j, t):
+            i = tok_sem(a, j, t, p)
+            part = spot.at[here]
+            peer = {"tensor": flip(y, 1, T)}
+            remote(part, part, tok_send.at[i], tok_recv.at[i], peer).wait_recv()
+
+    def tok_direct(a):
+        for j in sorted(bits_of(S)):
             tok_wait(a, j, 0)
             tok_forward(a, j)
+
+    def tok_passed(a):
+        for j in arrivals(S):
+            if j not in bits_of(S):
+                tok_wait(a, j, 0)
+                tok_forward(a, j)
 
     def tok_rest(a):
         tok_own(a).wait()
@@ -192,11 +225,12 @@
         return (m * S + k) * F + j
 
     def row_place(m, k, j):
-        return weights[m][1].at[at(flip(z, k, S) * F + flip(f, j, F), rows), :]
+        _, dst, first, size = weights[m]
+        return dst.at[at(flip(z, k, S) * F + flip(f, j, F), rows), first : first + size]
 
     def row_source(m, zd):
-        src, dst = weights[m]
-        return src.at[:, at(zd, dst.shape[1])]
+        src, dst, first, size = weights[m]
+        return src.at[:, pl.ds(pl.multiple_of(zd * dst.shape[1] + first, LANES), size)]
 
     def row_seq(m):
         for k in range(1, S):
@@ -270,19 +304,22 @@
         outs.append(copy)
 
     greet(S, T, F, z, y, f)
-    tok_forward(0, 0)
-    tok_own(0).start()
+    tok_seq(0, 0)
+    tok_tensor(0, 0)
+    for m in range(4):
+        row_forward(m, 0, 0)
+    for a in range(2):
+        tok_own(a).start()
+    for m in range(6):
+        row_own(m).start()
+
+    tok_direct(0)
     row_seq(0)
-    row_forward(0, 0, 0)
-    row_own(0).start()
-    tok_forward(1, 0)
-    tok_own(1).start()
-    for m in range(1, 4):
-        row_seq(m)
+    tok_passed(0)
+    row_seq(2)
+    tok_tensor(1, 0)
+    for m in (4, 5):
         row_forward(m, 0, 0)
-        row_own(m).start()
-
-    tok_seq(0)
     tok_rest(0)
     put(hid, hid_o)
     chunk = 32
@@ -311,6 +348,7 @@
         return (cos_in * cos_out - sin_in * sin_out, sin_in * cos_out + cos_in * sin_out)
 
     row_arrive(0)
+    tok_seq(1, 0)
     row_relay(0)
     row_rest(0)
     put(wq, wq_o)
@@ -330,13 +368,24 @@
     for zd in range(S):
         pair_forward(zd, 0)
 
-    tok_seq(1)
+    row_arrive(2)
+    row_seq(3)
+    tok_direct(1)
+    row_seq(1)
+    row_relay(2)
+    for j in arrivals(F):
+        if low_bit(j, F) > 1:
+            for zd in range(S):
+                pair_wait(zd, j)
+                pair_forward(zd, j)
+    tok_passed(1)
+    row_seq(4)
+    row_arrive(3)
     row_arrive(1)
     for j in arrivals(F):
-        for zd in range(S):
-            pair_wait(zd, j)
-            pair_forward(zd, j)
-    row_relay(1)
+        if low_bit(j, F) == 1:
+            for zd in range(S):
+                pair_wait(zd, j)
 
     qc = max(32, min(tok, tok * 2048 // keys))
 
@@ -366,13 +415,13 @@
         repeat(tok // qc, forward_chunk)
     put(attn, attn_o)
 
+    row_seq(5)
+    row_relay(1)
     tok_rest(1)
     put(cot, cot_o)
     row_rest(1)
     put(wp, wp_o)
     attn_grad[...] = bf(mm(cot[...], wp[...], 1, 0))
-    row_arrive(2)
-    row_relay(2)
     for zd in range(S):
         n = (zd + 1) * F * tok
 
@@ -427,25 +476,58 @@
                 peer = {"fsdp": flip(f, bit, F)}
                 start(remote(spot, part_in.at[i], part_send.at[j - 1], part_recv.at[i], peer))
 
+    def proj_sum(j):
+        total = jnp.concatenate(
+            [proj_full[at(zd * F + flip(f, j, F), rows), :] for zd in range(S)], axis=0
+        )
+        for b in fbits:
+            if b < low_bit(j, F):
+                i = slot_of(j, b, F)
+                spot = proj_in.at[i]
+                peer = {"fsdp": flip(f, b, F)}
+                remote(spot, spot, proj_send.at[i], proj_recv.at[i], peer).wait_recv()
+                total = total + f32(proj_in[i])
+        return total
+
+    def proj_stage(bit):
+        for j in range(1, F):
+            if low_bit(j, F) == bit:
+                proj_out[j - 1] = bf(proj_sum(j))
+                i = slot_of(j - bit, bit, F)
+                peer = {"fsdp": flip(f, bit, F)}
+                there = proj_in.at[i]
+                start(remote(proj_out.at[j - 1], there, proj_send.at[j - 1], proj_recv.at[i], peer))
+
     part_stage(fbits[0])
+    proj_full[...] = mm(cot[...], attn[...], 0, 0)
+    proj_stage(fbits[0])
+    row_arrive(4)
+    for bit in fbits[1:]:
+        part_stage(bit)
+    for bit in fbits[1:]:
+        proj_stage(bit)
     row_rest(2)
+
+    cols = wu.shape[1]
+
+    def up_strips(first):
+        for n in range(first // STRIP, (first + half) // STRIP):
+            strip = slice(n * STRIP, (n + 1) * STRIP)
+            mid = mm(mlp_in[...], wu[:, strip], 1, 0) + up_bias[
+                :, pl.ds(pl.multiple_of(z * cols + n * STRIP, STRIP), STRIP)
+            ]
+            cdf = 0.5 * (1.0 + lax.erf(mid * 0.7071067811865476))
+            active[:, strip] = bf(mid * cdf)
+            slope[:, strip] = cdf + mid * jnp.exp(-0.5 * mid * mid) * 0.3989422804014327
+
+    up_strips(0)
+    row_relay(3)
+    row_arrive(5)
+    row_rest(3)
     put(wu, wu_o)
-
-    cols = wu.shape[1]
-    for n in range(cols // STRIP):
-        strip = slice(n * STRIP, (n + 1) * STRIP)
-        mid = mm(mlp_in[...], wu[:, strip], 1, 0) + up_bias[
-            :, pl.ds(pl.multiple_of(z * cols + n * STRIP, STRIP), STRIP)
-        ]
-        cdf = 0.5 * (1.0 + lax.erf(mid * 0.7071067811865476))
-        active[:, strip] = bf(mid * cdf)
-        slope[:, strip] = cdf + mid * jnp.exp(-0.5 * mid * mid) * 0.3989422804014327
-        if n == 0:
-            for bit in fbits[1:]:
-                part_stage(bit)
+    up_strips(half)
     put(active, active_o)
     put(slope, slope_o)
-    row_arrive(3)
     total = part_sum(0)
     for zd in range(S):
         here = slice(zd * tok, (zd + 1) * tok)
@@ -453,8 +535,12 @@
         tg[here, HEAD_DIM : 2 * HEAD_DIM] = bf(turn(total[here, :HEAD_DIM], cos_part, -sin_part))
         tg[here, 2 * HEAD_DIM :] = bf(total[here, HEAD_DIM:])
     put(tg, tg_o)
-    row_relay(3)
-    row_rest(3)
+    row_relay(4)
+    proj[...] = bf(proj_sum(0))
+    put(proj, proj_o)
+    row_rest(4)
+    row_relay(5)
+    row_rest(5)
     put(wd, wd_o)
     for copy in outs:
         copy.wait()
@@ -475,7 +561,7 @@
     outs = [((ntok, D), small)] * 4 + [((2, ntok, LANES), wide)]
     outs += [((D, w.shape[1] // S), small) for w in arrays[2:]]
     outs += [((ntok, HEAD_DIM), small), ((ntok, ff), small), ((ntok, ff), wide)]
-    outs += [((ntok, 3 * HEAD_DIM), small)]
+    outs += [((ntok, 3 * HEAD_DIM), small), ((S * rows, HEAD_DIM), small)]
     n_part = max(F - 1, 1)
     scratch = outs + [
         ((ntok, HEAD_DIM), small),
@@ -485,6 +571,9 @@
         ((ntok, keys), small),
         ((ntok, LANES), wide),
         ((n_part, ntok, 2 * HEAD_DIM), small),
+        ((D, HEAD_DIM), wide),
+        ((n_part, S * rows, HEAD_DIM), small),
+        ((n_part, S * rows, HEAD_DIM), small),
     ]
     dma = pltpu.SemaphoreType.DMA
     any_spec = pl.BlockSpec(memory_space=pl.ANY)
@@ -496,14 +585,16 @@
         out_specs=[any_spec] * len(outs),
         scratch_shapes=[pltpu.VMEM(*o) for o in scratch]
         + [
-            dma((6,)),
+            dma((8,)),
             dma((len(outs),)),
-            dma((2 * S * T,)),
-            dma((2 * S * T,)),
-            dma((4 * S * F,)),
-            dma((4 * S * F,)),
+            dma((2 * S * T * TOKEN_PARTS,)),
+            dma((2 * S * T * TOKEN_PARTS,)),
+            dma((6 * S * F,)),
+            dma((6 * S * F,)),
             dma((S * F,)),
             dma((S * F,)),
+            dma((n_part,)),
+            dma((n_part,)),
             dma((n_part,)),
             dma((n_part,)),
         ],
@@ -513,14 +604,28 @@
     )(*arrays, *vectors, inner, outer)
 
 
+def second_units(ff):
+    half = ff // 2
+    return (
+        (0, 0, HEAD_DIM),
+        (1, 0, half),
+        (1, half, half),
+        (2, 0, 3 * HEAD_DIM),
+        (3, 0, half),
+        (3, half, half),
+    )
+
+
 def second_kernel(S, T, F, turned, *refs):
     cot_i, hid_i, attn_in_i, mlp_in_i, stat_i, wq_i, wp_i, wu_i, wd_i = refs[:9]
-    attn_i, active_i, slope_i, tg_i, own_cot, attn_gain, mlp_gain = refs[9:16]
-    grads, refs = refs[16:20], refs[20:]
+    attn_i, active_i, slope_i, tg_i, proj_i, own_cot, attn_gain, mlp_gain = refs[9:17]
+    grads, refs = refs[17:21], refs[21:]
     homes, (gain_o, qkv_bias_o, up_bias_o, out_bias_o), refs = refs[:2], refs[2:6], refs[6:]
     cot, hid, attn_in, mlp_in, stat, wq, wp, wud, attn, active, tg, pre = refs[:12]
     wide, own_half, sums, vec, vec_in, vec_seq, vec_ten = refs[12:19]
-    out_b, in_b, seq_b, refs = refs[19:23], refs[23:27], refs[27:31], refs[31:]
+    n_u = len(second_units(1))
+    out_b, in_b = (None, *refs[19 : 18 + n_u]), (None, *refs[18 + n_u : 17 + 2 * n_u])
+    seq_b, refs = refs[17 + 2 * n_u : 17 + 3 * n_u], refs[17 + 3 * n_u :]
     y_out, y_in, z_out, z_in, home_v = refs[:5]
     load_sem, own_sem, out_sem, in_sem, seq_send, seq_recv = refs[5:11]
     y_send, y_recv, z_send, z_recv, v_send, v_recv = refs[11:17]
@@ -529,12 +634,9 @@
     tok, width = homes[0].shape
     ntok, D = wide.shape
     ff = active.shape[1]
-    units = (
-        (attn, cot, HEAD_DIM),
-        (active, cot, ff),
-        (tg, attn_in, 3 * HEAD_DIM),
-        (pre, mlp_in, ff),
-    )
+    rights, lefts = (attn, active, tg, pre), (cot, cot, attn_in, mlp_in)
+    units = second_units(ff)
+    P1, D1, D2, Q1, U1, U2 = range(n_u)
     sends = []
 
     def start(copy):
@@ -555,11 +657,12 @@
                 waited.add(name)
                 loads[name].wait()
 
-    load("cot", cot_i, cot)
-    load("attn", attn_i, attn)
+    load("proj", proj_i, seq_b[0])
     load("active", active_i, active)
     load("wd", wd_i, wud)
+    load("attn", attn_i, attn)
     load("wp", wp_i, wp)
+    load("cot", cot_i, cot)
     load("slope", slope_i, wide.at[:, :ff])
     load("tg", tg_i, tg)
     load("attn_in", attn_in_i, attn_in)
@@ -571,8 +674,9 @@
     greet(S, T, F, z, y, f)
 
     def block_sum(u, j):
-        right, left, _ = units[u]
-        rows = grads[u].shape[0]
+        g, first, size = units[u]
+        right, left = rights[g].at[:, first : first + size], lefts[g]
+        rows = grads[g].shape[0]
         fd = flip(f, j, F)
         if turned:
             block = jnp.concatenate([left[at(zd * F + fd, rows), :] for zd in range(S)], axis=0)
@@ -605,23 +709,27 @@
                     )
                 )
 
+    def grad_place(u, zd):
+        g, first, size = units[u]
+        start_col = zd * rights[g].shape[1] + first
+        return grads[g].at[:, pl.ds(pl.multiple_of(start_col, LANES), size)]
+
     def own_grad(u):
-        rows = grads[u].shape[0]
-        cols = units[u][2]
-        return pltpu.make_async_copy(
-            seq_b[u].at[at(z, rows), :], grads[u].at[:, at(z, cols)], own_sem.at[u]
-        )
+        rows = grads[0].shape[0]
+        return pltpu.make_async_copy(seq_b[u].at[at(z, rows), :], grad_place(u, z), own_sem.at[u])
 
     def seq_stage(u):
-        rows = grads[u].shape[0]
-        cols = units[u][2]
-        seq_b[u][...] = bf(block_sum(u, 0))
+        rows = grads[0].shape[0]
+        if u == P1:
+            need("proj")
+        else:
+            seq_b[u][...] = bf(block_sum(u, 0))
         for k in range(1, S):
             peer = flip(z, k, S)
             start(
                 remote(
                     seq_b[u].at[at(peer, rows), :],
-                    grads[u].at[:, at(z, cols)],
+                    grad_place(u, z),
                     seq_send.at[u * S + k],
                     seq_recv.at[u * S + k],
                     {"seq": peer},
@@ -630,9 +738,8 @@
         own_grad(u).start()
 
     def seq_wait(u):
-        cols = units[u][2]
         for k in range(1, S):
-            spot = grads[u].at[:, at(flip(z, k, S), cols)]
+            spot = grad_place(u, flip(z, k, S))
             i = u * S + k
             remote(spot, spot, seq_send.at[i], seq_recv.at[i], {"seq": flip(z, k, S)}).wait_recv()
         own_grad(u).wait()
@@ -655,7 +762,7 @@
 
     def token_part(s, j):
         zd = flip(z, line_mask(j), S)
-        total = own_half[at(zd, tok), :]
+        total = own_half[s, at(zd, tok), :]
         for t in range(1, T):
             i = y_index(s, t, 0) + j
             spot = y_in.at[i]
@@ -680,7 +787,7 @@
                 start(remote(z_out.at[i], z_in.at[there], z_send.at[i], z_recv.at[there], peer))
 
     def home_copy(s):
-        return pltpu.make_async_copy(home_v.at[s], homes[s], own_sem.at[4 + s])
+        return pltpu.make_async_copy(home_v.at[s], homes[s], own_sem.at[n_u + s])
 
     def token_home(s):
         home_v[s] = token_part(s, 0)
@@ -732,31 +839,40 @@
             parts = [a + b for a, b in zip(parts[::2], parts[1::2])]
         gain_o[...] = parts[0]
 
-    need("cot", "attn")
+    first_stage = lambda u: fsdp_stage(u, fbits[0])
+
+    def later_stages(u):
+        for bit in fbits[1:]:
+            fsdp_stage(u, bit)
+
+    def later_tokens(s):
+        for bit in sbits[1:]:
+            token_stage(s, bit)
+
+    def half_strips(s, t, term):
+        for n in range(width // STRIP):
+            there = pl.ds(pl.multiple_of(flip(y, t, T) * width + n * STRIP, STRIP), STRIP)
+            here = slice(n * STRIP, (n + 1) * STRIP)
+            if t:
+                y_store(s, t, here, term(there))
+            else:
+                own_half[s, :, here] = term(there)
+
+    seq_stage(P1)
     vec[0] = jnp.zeros(vec.shape[1:], jnp.float32)
-    fsdp_stage(0, fbits[0])
-    need("active", "wd", "wp")
+    need("active", "wd", "attn", "wp")
 
     def branch(column):
         return mm(active[...], wud[column, :], 1, 1) + mm(attn[...], wp[column, :], 1, 1)
 
-    for t in [*range(1, T), 0]:
-        for n in range(width // STRIP):
-            there = pl.ds(
-                pl.multiple_of(flip(y, t, T) * width + n * STRIP, STRIP), STRIP
-            )
-            here = slice(n * STRIP, (n + 1) * STRIP)
-            if t:
-                y_store(0, t, here, branch(there))
-            else:
-                own_half[:, here] = branch(there)
-        if t == T - 1:
-            tensor_send(0)
-    for bit in fbits[1:]:
-        fsdp_stage(0, bit)
-    fsdp_stage(1, fbits[0])
-    seq_stage(0)
-    token_stage(0, sbits[0])
+    for t in range(1, T):
+        half_strips(0, t, branch)
+    tensor_send(0)
+    need("cot")
+    first_stage(D1)
+    half_strips(0, 0, branch)
+    later_stages(D1)
+    first_stage(D2)
 
     need("slope")
     for n in range(ff // STRIP):
@@ -765,16 +881,13 @@
         vec[0, 5:6, here] = jnp.sum(value, axis=0, keepdims=True)
         pre[:, here] = bf(value)
     load("wu", wu_i, wud)
-    for bit in fbits[1:]:
-        fsdp_stage(1, bit)
-    for bit in sbits[1:]:
-        token_stage(0, bit)
+    token_stage(0, sbits[0])
     need("tg", "attn_in")
-    fsdp_stage(2, fbits[0])
-    seq_stage(1)
+    first_stage(Q1)
+    later_stages(D2)
     need("mlp_in")
-    fsdp_stage(3, fbits[0])
-    token_home(0)
+    first_stage(U1)
+    first_stage(U2)
 
     need("wu", "wq", "hid", "stat")
     lane_parts = range(0, STRIP, LANES)
@@ -800,8 +913,8 @@
     vec[0, 4:5, : 3 * HEAD_DIM] = jnp.sum(f32(tg[...]), axis=0, keepdims=True)
     vec[0, 6:7, :width] = jnp.sum(f32(own_cot[...]), axis=0, keepdims=True)
     vec_fsdp(0)
-    for bit in fbits[1:]:
-        fsdp_stage(2, bit)
+    seq_stage(D1)
+    later_stages(Q1)
     sums[0] = jnp.broadcast_to(jnp.sum(sums[0], axis=-1, keepdims=True) / D, sums.shape[1:])
     sums[1] = jnp.broadcast_to(jnp.sum(sums[1], axis=-1, keepdims=True) / D, sums.shape[1:])
 
@@ -810,38 +923,35 @@
         xhat = (f32(hid[:, column]) - mean) * inv_std
         return inv_std * (wide[:, column] - sums[0, :, :1] - xhat * sums[1, :, :1])
 
-    for t in [*range(1, T), 0]:
-        for n in range(width // STRIP):
-            there = pl.ds(
-                pl.multiple_of(flip(y, t, T) * width + n * STRIP, STRIP), STRIP
-            )
-            here = slice(n * STRIP, (n + 1) * STRIP)
-            if t:
-                y_store(1, t, here, input_term(there))
-            else:
-                own_half[:, here] = input_term(there)
-        if t == T - 1:
-            tensor_send(1)
+    for t in range(1, T):
+        half_strips(1, t, input_term)
+    tensor_send(1)
+    half_strips(1, 0, input_term)
+    later_tokens(0)
+    seq_stage(D2)
+    later_stages(U1)
     vec_fsdp_sum(0)
     for b in range(1, n_fsdp):
         vec_fsdp(b)
-        if b == 1:
-            seq_stage(2)
-            for bit in fbits[1:]:
-                fsdp_stage(3, bit)
-        vec_fsdp_sum(b)
+        if b < n_fsdp - 1:
+            vec_fsdp_sum(b)
+    seq_stage(Q1)
+    later_stages(U2)
+    token_stage(1, sbits[0])
+    token_home(0)
+    seq_stage(U1)
+    if n_fsdp > 1:
+        vec_fsdp_sum(n_fsdp - 1)
     for k in range(1, S):
         start(vec_seq_copy(k))
-    token_stage(1, sbits[0])
-    seq_stage(3)
+    seq_stage(U2)
+    later_tokens(1)
     vec_seq_sum()
     for t in range(1, T):
         start(vec_ten_copy(t))
-    for bit in sbits[1:]:
-        token_stage(1, bit)
     vec_ten_sum()
     token_home(1)
-    for u in range(4):
+    for u in range(n_u):
         seq_wait(u)
     for s in range(2):
         home_copy(s).wait()
@@ -850,7 +960,7 @@
 
 
 def second_call(S, T, F, first, own_cot, attn_gain, mlp_gain, rows):
-    hid, cot, attn_in, mlp_in, stat, wq, wp, wu, wd, attn, active, slope, tg = first
+    hid, cot, attn_in, mlp_in, stat, wq, wp, wu, wd, attn, active, slope, tg, proj = first
     turned = rows % LANES != 0
     if turned:
         cot, attn_in, mlp_in = cot.T, attn_in.T, mlp_in.T
@@ -860,7 +970,7 @@
     small, wide = jnp.bfloat16, jnp.float32
     cols = (HEAD_DIM, ff, 3 * HEAD_DIM, ff)
     parts, block, n_f = max(F - 1, 1), S * rows, F.bit_length() - 1
-    ins = (cot, hid, attn_in, mlp_in, stat, wq, wp, wu, wd, attn, active, slope, tg)
+    ins = (cot, hid, attn_in, mlp_in, stat, wq, wp, wu, wd, attn, active, slope, tg, proj)
     any_spec = pl.BlockSpec(memory_space=pl.ANY)
     vmem = pl.BlockSpec(memory_space=pltpu.VMEM)
     dma = pltpu.SemaphoreType.DMA
@@ -870,15 +980,17 @@
     scratch += [
         ((ntok, ff), small),
         ((ntok, D), wide),
-        ((ntok, width), wide),
+        ((2, ntok, width), wide),
         ((2, ntok, LANES), wide),
         ((n_f + 1, 8, D), wide),
         ((n_f, 8, D), wide),
         ((max(S - 1, 1), 8, D), wide),
         ((T, 4, D), wide),
     ]
-    scratch += [((parts, block, c), small) for c in cols] * 2
-    scratch += [((block, c), small) for c in cols]
+    chunks = [size for _, _, size in second_units(ff)]
+    n_u = len(chunks)
+    scratch += [((parts, block, c), small) for c in chunks[1:]] * 2
+    scratch += [((block, c), small) for c in chunks]
     n_y, n_z, n_v = 2 * max(T - 1, 1) * S, 2 * max(S - 1, 1), n_f + S + T
     scratch += [((n_y, tok, width), small)] * 2 + [((n_z, tok, width), small)] * 2
     scratch += [((2, tok, width), wide)]
@@ -893,11 +1005,11 @@
         scratch_shapes=[pltpu.VMEM(*s) for s in scratch]
         + [
             dma((len(ins),)),
-            dma((6,)),
-            dma((4 * parts,)),
-            dma((4 * parts,)),
-            dma((4 * S,)),
-            dma((4 * S,)),
+            dma((n_u + 2,)),
+            dma((n_u * parts,)),
+            dma((n_u * parts,)),
+            dma((n_u * S,)),
+            dma((n_u * S,)),
             dma((n_y,)),
             dma((n_y,)),
             dma((n_z,)),

time: 340 us -> 277 us (0.81)
  Pallas kernels: 329 us -> 265 us
    pallas_call x1, Pallas kernels: 193 us -> 140 us  [first_call(): pl.pallas_call(functools.partial(first_kernel, S, T, F), out_shape=[jax.S...]
    pallas_call x1, Pallas kernels: 136 us -> 125 us  [second_call(): pl.pallas_call(functools.partial(second_kernel, S, T, F, turned), out_sha...]
where the time goes in v1:
time: 277 us; the launch traced here: 276 us
  Pallas kernels  265 us (96%)
  other arithmetic  7.58 us (3%)
  local copies, waits for them, and re-layouts  3.05 us (1%)
    pallas_call x1, Pallas kernels, first_call(): pl.pallas_call(functools.partial(first_kernel, S, T, F), out_shape=[jax.S...  140 us
    pallas_call x1, Pallas kernels, second_call(): pl.pallas_call(functools.partial(second_kernel, S, T, F, turned), out_sha...  125 us

profile of v1, /device:TPU:8, one launch (start us, length us, event | category | flops | bytes accessed | tf_op | source)
XLA Modules:
  0.0 276.1 jit_solution(12919395723230084551)
XLA Ops:
  0.6 140.3 %shard_map.263 = (bf16[512,2048]{1,0:T(8,128)(2,1)}, bf16[512,2048]{1,0:T(8,128)(2,1)}, bf16[512,2048]{1,0:T(8,128)(2,1)}, bf16[512,2048]{1,0:T(8,128)(2,1)}, f3...) custom-call(bf16[128,1024]{1,0:T(8,128)(2,1)} %refs_0_.1, ...), custom_call_target="tpu_custom_call" | custom-call | tf_op jit(solution)/shard_map/pallas_call | solution.py:581
  140.9 124.5 %shard_map.264 = (bf16[128,1024]{1,0:T(8,128)(2,1)}, bf16[128,4096]{1,0:T(8,128)(2,1)}, bf16[128,3072]{1,0:T(8,128)(2,1)}, bf16[128,4096]{1,0:T(8,128)(2,1)}, f3...) custom-call(bf16[512,2048]{1,0:T(8,128)(2,1)} %get-tuple-element.38., ...), custom_call_target="tpu_custom_call" | custom-call | tf_op jit(solution)/shard_map/pallas_call | solution.py:997
  265.5 0.0 copy-start.4
  265.5 0.0 copy-start.3
  265.5 0.0 copy-start.2
  265.5 2.4 add_convert_fusion
  267.9 0.0 copy-start.1
  267.9 0.0 copy-done.4
  267.9 0.6 fusion
  268.5 0.0 copy-done.3
  268.5 0.8 convert_element_type.29
  269.4 0.0 copy-done.2
  269.4 1.3 convert_element_type.28
  270.7 0.0 copy-done.1
  270.7 0.0 copy-start
  270.7 1.5 convert_element_type.30
  272.2 0.0 copy-done
  272.2 0.0 copy-start.6
  272.2 0.0 copy-start.7
  272.2 0.0 copy-start.5
  272.2 1.5 convert_element_type.31
  273.7 0.0 copy-done.6
  273.7 0.6 copy.34
  274.3 0.0 copy-done.7
  274.3 0.6 copy.35
  274.9 0.6 copy.36
  275.5 0.0 copy-done.5
  275.5 0.6 copy.37
Async XLA Ops:
  265.5 2.4 copy-start.4
  265.5 3.0 %copy-start.3 = (bf16[128,1024]{1,0:T(8,128)(2,1)S(1)}, bf16[128,1024]{1,0:T(8,128)(2,1)}, u32[]{:S(2)}) copy-start(bf16[128,1024]{1,0:T(8,128)(2,1)} %get-tuple-element.57) | copy-start | bytes 786436
  265.5 3.9 %copy-start.2 = (bf16[128,3072]{1,0:T(8,128)(2,1)S(1)}, bf16[128,3072]{1,0:T(8,128)(2,1)}, u32[]{:S(2)}) copy-start(bf16[128,3072]{1,0:T(8,128)(2,1)} %get-tuple-element.55) | copy-start | bytes 2359300
  267.9 2.8 %copy-start.1 = (bf16[128,4096]{1,0:T(8,128)(2,1)S(1)}, bf16[128,4096]{1,0:T(8,128)(2,1)}, u32[]{:S(2)}) copy-start(bf16[128,4096]{1,0:T(8,128)(2,1)} %get-tuple-element.59) | copy-start | bytes 3145732
  270.7 1.5 copy-start
  272.2 1.5 copy-start.6
  272.2 2.1 copy-start.7
  272.2 3.3 %copy-start.5 = (f32[1,4096]{1,0:T(1,128)S(1)}, f32[1,4096]{1,0:T(1,128)}, u32[]{:S(2)}) copy-start(f32[1,4096]{1,0:T(1,128)} %get-tuple-element.60) | copy-start | bytes 49156
